TPU v7x, 32 devices: a whole 2x2x4 slice. The times are simulated.
32 devices in a mesh: sub: 4 (over x, core), gx: 4 (over z), gy: 2 (over y).
Axes of the slice: x: 2, y: 2, z: 4, core: 2. Of those that a mesh axis runs over, the one named last changes fastest.
Arguments:
- state: float32 [4, 256, 512], P(None, ('sub', 'gx'), 'gy'), may hold values from -4 to 4
- damping: float32 [4, 256, 512], P(None, ('sub', 'gx'), 'gy'), may hold values from 0.005 to 0.1
- weights: float32 [4], replicated, may hold values from 0.5 to 1.5
Outputs:
- combined: float32 [4, 256, 512], P(None, ('sub', 'gx'), 'gy')
- column_error: float32 [4, 512], P(None, 'gy')
All inputs are finite; a program needn't handle non-finite values.
Results may differ from a plain program's by a relative error of at most 0.0003.
Values sent between devices are 32-bit elements; how exact they have to be, the bound alone decides.
No kernel may reach another device: no remote copies, remote signals or barrier semaphores. Data moves between devices by JAX's collectives and lax.ppermute only.
A program may use at most 64 MiB of HBM per device.

v0:
```python
import jax
import jax.numpy as jnp
from jax import lax
from jax.sharding import PartitionSpec as P

KRYLOV = 12
SUBSTEPS = 4
dt_total = 4.0
sound_sq = 1.0
buoyancy_sq = 0.5
norm_eps = 1e-06
taylor_degree = 12
squarings = 8


def padded(cells, sides, width):
    for axis, dim in sides:
        count = lax.axis_size(axis)
        ends = count - 1
        head = lax.slice_in_dim(cells, 0, width, axis=dim)
        tail = lax.slice_in_dim(cells, cells.shape[dim] - width, cells.shape[dim], axis=dim)
        cells = jnp.concatenate(
            [
                lax.ppermute(tail, axis, [(i, (i + 1) % count) for i in range(ends)]),
                cells,
                lax.ppermute(head, axis, [((i + 1) % count, i) for i in range(ends)]),
            ],
            axis=dim,
        )
    return cells


def wave(field):
    row_pair = jnp.stack([field[0], field[3]])
    column_pair = jnp.stack([field[1], field[3]])
    rows_padded = padded(row_pair, ((("sub", "gx"), 1),), 1)
    columns_padded = padded(column_pair, (("gy", 2),), 1)
    rise_x = 0.5 * (rows_padded[1, 2:, :] - rows_padded[1, :-2, :])
    rise_y = 0.5 * (columns_padded[1, :, 2:] - columns_padded[1, :, :-2])
    spread = 0.5 * (rows_padded[0, 2:, :] - rows_padded[0, :-2, :]) + 0.5 * (
        columns_padded[0, :, 2:] - columns_padded[0, :, :-2]
    )
    return jnp.stack([-rise_x, -rise_y + field[2], -buoyancy_sq * field[1], -sound_sq * spread])


def phi_first(hessenberg):
    extent = hessenberg.shape[0]
    augmented = jnp.zeros((extent + 1, extent + 1), jnp.float32)
    augmented = augmented.at[:extent, :extent].set(hessenberg).at[0, extent].set(1.0)
    scaled = augmented / 2.0**squarings
    result = jnp.eye(extent + 1, dtype=jnp.float32)
    power_term = result
    for degree in range(1, taylor_degree + 1):
        power_term = jnp.dot(power_term, scaled, precision=lax.Precision.HIGHEST) / degree
        result = result + power_term
    for repeat in range(squarings):
        result = jnp.dot(result, result, precision=lax.Precision.HIGHEST)
    return result[:extent, extent]


def arnoldi(start, stiffness):
    shape = start.shape
    basis = jnp.zeros((KRYLOV + 1, start.size), jnp.float32).at[0].set(start.reshape(-1))
    hessenberg = jnp.zeros((KRYLOV + 1, KRYLOV), jnp.float32)
    for column in range(KRYLOV):
        current = basis[column].reshape(shape)
        image = (dt_total * (wave(current) - stiffness * current)).reshape(-1)
        partial_value = jnp.dot(basis[: column + 1], image, precision=lax.Precision.HIGHEST)
        products, squared = lax.psum((partial_value, jnp.sum(image * image)), ("sub", "gx", "gy"))
        image = image - jnp.dot(products, basis[: column + 1], precision=lax.Precision.HIGHEST)
        length = jnp.sqrt(jnp.maximum(squared - jnp.sum(products * products), 0.0) + norm_eps)
        hessenberg = (
            hessenberg.at[: column + 1, column].set(products).at[column + 1, column].set(length)
        )
        basis = basis.at[column + 1].set(image / length)
    return (basis, hessenberg)


def shards(state, damping, weights):
    stiffness = 3.0 * damping * state * state
    forcing = wave(state) - damping * state * state * state
    beta_norm = jnp.sqrt(lax.psum(jnp.sum(forcing * forcing), ("sub", "gx", "gy")) + norm_eps)
    basis, hessenberg = arnoldi(forcing / beta_norm, stiffness)
    mixing = jnp.zeros((KRYLOV,), jnp.float32)
    highest = jnp.zeros((), jnp.float32)
    for member in range(SUBSTEPS):
        fraction = (member + 1) / SUBSTEPS
        factor = dt_total * fraction
        coefficients = phi_first(fraction * hessenberg[:KRYLOV])
        mixing = mixing + weights[member] * factor * beta_norm * coefficients
        estimate = (
            factor
            * beta_norm
            * fraction
            * hessenberg[KRYLOV, KRYLOV - 1]
            * jnp.abs(coefficients[KRYLOV - 1])
        )
        highest = jnp.maximum(highest, estimate)
    increment = jnp.dot(mixing, basis[:KRYLOV], precision=lax.Precision.HIGHEST)
    combined = state + increment.reshape(state.shape)
    local_peak = highest * jnp.max(jnp.abs(basis[KRYLOV].reshape(state.shape)), axis=1)
    column_error = lax.pmax(local_peak, ("sub", "gx"))
    return (combined, column_error)


def solution(mesh):
    return jax.shard_map(
        shards,
        mesh=mesh,
        in_specs=(P(None, ("sub", "gx"), "gy"), P(None, ("sub", "gx"), "gy"), P()),
        out_specs=(P(None, ("sub", "gx"), "gy"), P(None, "gy")),
        check_vma=False,
    )
```

profile of v0, /device:TPU:0, one launch (start us, length us, event | category | flops | bytes accessed | tf_op | source)
XLA Modules:
  0.0 885.9 jit_solution(2977581656855364826)
XLA Ops:
  2.7 4.9 collective-permute-start.3
  23.8 5.2 collective-permute-start.1
  33.7 41.0 %psum.175 = f32[]{:T(128)} all-reduce(f32[]{:T(128)} %get-tuple-element.640), channel_id=1, replica_groups=mesh['sub'=4,'gx'=4,'gy'=2] {'sub','gx','gy'}, use_global_device_ids=true, to_apply=%region_1.0 | all-reduce | flops 1 | bytes 8 | tf_op jit(solution)/shard_map/psum | solution.py:82
  77.1 4.7 collective-permute-start.5
  83.1 4.5 collective-permute-start.7
  89.8 42.5 %all-reduce.17 = (f32[]{:T(128)}, f32[1]{0:T(128)}) all-reduce(f32[]{:T(128)} %get-tuple-element.587, f32[1]{0:T(128)} %bitcast.1), channel_id=1, replica_groups=mesh['sub'=4,'gx'=4,'gy'=2] {'sub','gx','gy'}, use_global_device_ids=true, to_apply=%region_4.0 | all-reduce | flops 2 | bytes 16 | tf_op jit(solution)/shard_map/psum | solution.py:69
  136.6 4.5 collective-permute-start.9
  142.5 4.5 collective-permute-start.11
  150.5 41.8 %all-reduce.16 = (f32[2]{0:T(128)S(1)}, f32[]{:T(128)}) all-reduce(f32[2]{0:T(128)S(1)} %convolution_bitcast_fusion.10, f32[]{:T(128)} %get-tuple-element.636), channel_id=1, replica_groups=mesh['sub'=4,'gx'=4,'gy'=2] {'sub','gx','gy'}, use_global_device_ids=true, to_apply=%region_6.0 | all-reduce | flops 3 | bytes 24 | tf_op jit(solution)/shard_map/psum | solution.py:69
  197.9 4.7 collective-permute-start.13
  204.5 4.5 collective-permute-start.15
  213.2 41.8 %all-reduce.15 = (f32[3]{0:T(128)S(1)}, f32[]{:T(128)}) all-reduce(f32[3]{0:T(128)S(1)} %convolution_bitcast_fusion.9, f32[]{:T(128)} %get-tuple-element.634), channel_id=1, replica_groups=mesh['sub'=4,'gx'=4,'gy'=2] {'sub','gx','gy'}, use_global_device_ids=true, to_apply=%region_11.0 | all-reduce | flops 4 | bytes 32 | tf_op jit(solution)/shard_map/psum | solution.py:69
  260.5 4.5 collective-permute-start.17
  267.0 4.5 collective-permute-start.19
  275.9 41.0 %all-reduce.14 = (f32[4]{0:T(128)S(1)}, f32[]{:T(128)}) all-reduce(f32[4]{0:T(128)S(1)} %convolution_bitcast_fusion.8, f32[]{:T(128)} %get-tuple-element.632), channel_id=1, replica_groups=mesh['sub'=4,'gx'=4,'gy'=2] {'sub','gx','gy'}, use_global_device_ids=true, to_apply=%region_16.0 | all-reduce | flops 5 | bytes 40 | tf_op jit(solution)/shard_map/psum | solution.py:69
  322.4 4.7 collective-permute-start.21
  327.0 2.0 broadcast_select_fusion.8
  329.1 4.5 collective-permute-start.23
  337.8 41.8 %all-reduce.13 = (f32[5]{0:T(128)S(1)}, f32[]{:T(128)}) all-reduce(f32[5]{0:T(128)S(1)} %convolution_bitcast_fusion.7, f32[]{:T(128)} %get-tuple-element.630), channel_id=1, replica_groups=mesh['sub'=4,'gx'=4,'gy'=2] {'sub','gx','gy'}, use_global_device_ids=true, to_apply=%region_21.0 | all-reduce | flops 6 | bytes 48 | tf_op jit(solution)/shard_map/psum | solution.py:69
  385.0 4.5 collective-permute-start.25
  391.5 4.5 collective-permute-start.27
  400.2 41.1 %all-reduce.12 = (f32[6]{0:T(128)S(1)}, f32[]{:T(128)}) all-reduce(f32[6]{0:T(128)S(1)} %convolution_bitcast_fusion.6, f32[]{:T(128)} %get-tuple-element.628), channel_id=1, replica_groups=mesh['sub'=4,'gx'=4,'gy'=2] {'sub','gx','gy'}, use_global_device_ids=true, to_apply=%region_26.0 | all-reduce | flops 7 | bytes 56 | tf_op jit(solution)/shard_map/psum | solution.py:69
  446.9 4.7 collective-permute-start.29
  451.5 2.0 broadcast_select_fusion.6
  453.6 4.5 collective-permute-start.31
  462.3 42.2 %all-reduce.11 = (f32[7]{0:T(128)S(1)}, f32[]{:T(128)}) all-reduce(f32[7]{0:T(128)S(1)} %convolution_bitcast_fusion.5, f32[]{:T(128)} %get-tuple-element.626), channel_id=1, replica_groups=mesh['sub'=4,'gx'=4,'gy'=2] {'sub','gx','gy'}, use_global_device_ids=true, to_apply=%region_31.0 | all-reduce | flops 8 | bytes 64 | tf_op jit(solution)/shard_map/psum | solution.py:69
  510.0 4.5 collective-permute-start.33
  514.5 2.0 broadcast_select_fusion.5
  516.6 4.5 collective-permute-start.35
  525.3 41.1 %all-reduce.10 = (f32[8]{0:T(128)S(1)}, f32[]{:T(128)}) all-reduce(f32[8]{0:T(128)S(1)} %convolution_bitcast_fusion.4, f32[]{:T(128)} %get-tuple-element.624), channel_id=1, replica_groups=mesh['sub'=4,'gx'=4,'gy'=2] {'sub','gx','gy'}, use_global_device_ids=true, to_apply=%region_36.0 | all-reduce | flops 9 | bytes 72 | tf_op jit(solution)/shard_map/psum | solution.py:69
  571.9 4.7 collective-permute-start.37
  578.5 4.5 collective-permute-start.39
  587.3 41.8 %all-reduce.9 = (f32[9]{0:T(128)S(1)}, f32[]{:T(128)}) all-reduce(f32[9]{0:T(128)S(1)} %convolution_bitcast_fusion.3, f32[]{:T(128)} %get-tuple-element.622), channel_id=1, replica_groups=mesh['sub'=4,'gx'=4,'gy'=2] {'sub','gx','gy'}, use_global_device_ids=true, to_apply=%region_41.0 | all-reduce | flops 10 | bytes 80 | tf_op jit(solution)/shard_map/psum | solution.py:69
  634.7 4.5 collective-permute-start.41
  641.2 4.5 collective-permute-start.43
  650.0 41.3 %all-reduce.8 = (f32[10]{0:T(128)S(1)}, f32[]{:T(128)}) all-reduce(f32[10]{0:T(128)S(1)} %convolution_bitcast_fusion.2, f32[]{:T(128)} %get-tuple-element.620), channel_id=1, replica_groups=mesh['sub'=4,'gx'=4,'gy'=2] {'sub','gx','gy'}, use_global_device_ids=true, to_apply=%region_46.0 | all-reduce | flops 11 | bytes 88 | tf_op jit(solution)/shard_map/psum | solution.py:69
  696.9 4.7 collective-permute-start.45
  701.5 2.0 broadcast_select_fusion.2
  703.5 4.5 collective-permute-start.47
  712.4 41.8 %all-reduce.7 = (f32[11]{0:T(128)S(1)}, f32[]{:T(128)}) all-reduce(f32[11]{0:T(128)S(1)} %convolution_bitcast_fusion.1, f32[]{:T(128)} %get-tuple-element.618), channel_id=1, replica_groups=mesh['sub'=4,'gx'=4,'gy'=2] {'sub','gx','gy'}, use_global_device_ids=true, to_apply=%region_51.0 | all-reduce | flops 12 | bytes 96 | tf_op jit(solution)/shard_map/psum | solution.py:69
  759.7 4.5 collective-permute-start.49
  766.2 4.5 collective-permute-start.51
  775.4 40.7 %all-reduce.6 = (f32[12]{0:T(128)S(1)}, f32[]{:T(128)}) all-reduce(f32[12]{0:T(128)S(1)} %convolution_bitcast_fusion, f32[]{:T(128)} %get-tuple-element.616), channel_id=1, replica_groups=mesh['sub'=4,'gx'=4,'gy'=2] {'sub','gx','gy'}, use_global_device_ids=true, to_apply=%region_56.0 | all-reduce | flops 13 | bytes 104 | tf_op jit(solution)/shard_map/psum | solution.py:69
  820.2 2.5 fusion.334
  822.7 2.6 fusion.336
  827.2 2.0 scatter.214
  839.3 2.0 scatter.206
  851.6 32.4 %pmax.7 = f32[4,256]{1,0:T(4,128)} all-reduce(f32[4,256]{1,0:T(4,128)S(1)} %broadcast_multiply_fusion.68), channel_id=1, replica_groups=mesh['sub'=4,'gx'=4,'gy'=2] {'sub','gx'}, use_global_device_ids=true, to_apply=%region_62.0 | all-reduce | flops 1024 | bytes 8192 | tf_op jit(solution)/shard_map/pmax | solution.py:102
  (511 shorter events, 150.8 us)
Async XLA Ops:
  1.4 20.9 %collective-permute-start.2 = (f32[2,16,1]{2,1,0:T(8,128)S(1)}, f32[2,16,1]{2,1,0:T(8,128)S(1)}, u32[]{:S(2)}, u32[]{:S(2)}) collective-permute-start(f32[2,16,1]{2,1,0:T(8,128)S(1)} %get-tuple-element.735), channel_id=1, source_target_pairs={{1,0},{3,2},{5,4},{7,6},{9,8},{11,10},{13,12},{15,14},{17,16},{19,... | collective-permute-start | bytes 392 | tf_op jit(solution)/shard_map/ppermute | solution.py:26
  2.7 19.7 %collective-permute-start.3 = (f32[2,16,1]{2,1,0:T(8,128)S(1)}, f32[2,16,1]{2,1,0:T(8,128)S(1)}, u32[]{:S(2)}, u32[]{:S(2)}) collective-permute-start(f32[2,16,1]{2,1,0:T(8,128)S(1)} %get-tuple-element.736), channel_id=1, source_target_pairs={{0,1},{2,3},{4,5},{6,7},{8,9},{10,11},{12,13},{14,15},{16,17},{18,... | collective-permute-start | bytes 392 | tf_op jit(solution)/shard_map/ppermute | solution.py:24
  22.5 10.5 %collective-permute-start = (f32[2,1,256]{2,1,0:T(1,128)S(1)}, f32[2,1,256]{2,1,0:T(1,128)S(1)}, u32[]{:S(2)}, u32[]{:S(2)}) collective-permute-start(f32[2,1,256]{2,1,0:T(1,128)S(1)} %get-tuple-element.733), channel_id=1, source_target_pairs={{2,0},{4,2},{6,4},{8,6},{10,8},{12,10},{14,12},{16,14},{18,16},{20... | collective-permute-start | bytes 6152 | tf_op jit(solution)/shard_map/ppermute | solution.py:26
  23.8 9.2 %collective-permute-start.1 = (f32[2,1,256]{2,1,0:T(1,128)S(1)}, f32[2,1,256]{2,1,0:T(1,128)S(1)}, u32[]{:S(2)}, u32[]{:S(2)}) collective-permute-start(f32[2,1,256]{2,1,0:T(1,128)S(1)} %get-tuple-element.734), channel_id=1, source_target_pairs={{0,2},{2,4},{4,6},{6,8},{8,10},{10,12},{12,14},{14,16},{16,18},{18... | collective-permute-start | bytes 6152 | tf_op jit(solution)/shard_map/ppermute | solution.py:24
  75.8 13.3 %collective-permute-start.4 = (f32[2,1,256]{2,1,0:T(1,128)S(1)}, f32[2,1,256]{2,1,0:T(1,128)S(1)}, u32[]{:S(2)}, u32[]{:S(2)}) collective-permute-start(f32[2,1,256]{2,1,0:T(1,128)S(1)} %get-tuple-element.729), channel_id=1, source_target_pairs={{2,0},{4,2},{6,4},{8,6},{10,8},{12,10},{14,12},{16,14},{18,16},{20... | collective-permute-start | bytes 6152 | tf_op jit(solution)/shard_map/ppermute | solution.py:26
  77.1 12.0 %collective-permute-start.5 = (f32[2,1,256]{2,1,0:T(1,128)S(1)}, f32[2,1,256]{2,1,0:T(1,128)S(1)}, u32[]{:S(2)}, u32[]{:S(2)}) collective-permute-start(f32[2,1,256]{2,1,0:T(1,128)S(1)} %get-tuple-element.730), channel_id=1, source_target_pairs={{0,2},{2,4},{4,6},{6,8},{8,10},{10,12},{12,14},{14,16},{16,18},{18... | collective-permute-start | bytes 6152 | tf_op jit(solution)/shard_map/ppermute | solution.py:24
  135.3 13.2 %collective-permute-start.8 = (f32[2,1,256]{2,1,0:T(1,128)S(1)}, f32[2,1,256]{2,1,0:T(1,128)S(1)}, u32[]{:S(2)}, u32[]{:S(2)}) collective-permute-start(f32[2,1,256]{2,1,0:T(1,128)S(1)} %get-tuple-element.725), channel_id=1, source_target_pairs={{2,0},{4,2},{6,4},{8,6},{10,8},{12,10},{14,12},{16,14},{18,16},{20... | collective-permute-start | bytes 6152 | tf_op jit(solution)/shard_map/ppermute | solution.py:26
  136.6 11.9 %collective-permute-start.9 = (f32[2,1,256]{2,1,0:T(1,128)S(1)}, f32[2,1,256]{2,1,0:T(1,128)S(1)}, u32[]{:S(2)}, u32[]{:S(2)}) collective-permute-start(f32[2,1,256]{2,1,0:T(1,128)S(1)} %get-tuple-element.726), channel_id=1, source_target_pairs={{0,2},{2,4},{4,6},{6,8},{8,10},{10,12},{12,14},{14,16},{16,18},{18... | collective-permute-start | bytes 6152 | tf_op jit(solution)/shard_map/ppermute | solution.py:24
  141.2 7.2 collective-permute-start.10
  195.3 15.9 %collective-permute-start.14 = (f32[2,16,1]{2,1,0:T(8,128)S(1)}, f32[2,16,1]{2,1,0:T(8,128)S(1)}, u32[]{:S(2)}, u32[]{:S(2)}) collective-permute-start(f32[2,16,1]{2,1,0:T(8,128)S(1)} %get-tuple-element.723), channel_id=1, source_target_pairs={{1,0},{3,2},{5,4},{7,6},{9,8},{11,10},{13,12},{15,14},{17,16},{19,... | collective-permute-start | bytes 392 | tf_op jit(solution)/shard_map/ppermute | solution.py:26
  196.6 14.6 %collective-permute-start.12 = (f32[2,1,256]{2,1,0:T(1,128)S(1)}, f32[2,1,256]{2,1,0:T(1,128)S(1)}, u32[]{:S(2)}, u32[]{:S(2)}) collective-permute-start(f32[2,1,256]{2,1,0:T(1,128)S(1)} %get-tuple-element.721), channel_id=1, source_target_pairs={{2,0},{4,2},{6,4},{8,6},{10,8},{12,10},{14,12},{16,14},{18,16},{20... | collective-permute-start | bytes 6152 | tf_op jit(solution)/shard_map/ppermute | solution.py:26
  197.9 13.3 %collective-permute-start.13 = (f32[2,1,256]{2,1,0:T(1,128)S(1)}, f32[2,1,256]{2,1,0:T(1,128)S(1)}, u32[]{:S(2)}, u32[]{:S(2)}) collective-permute-start(f32[2,1,256]{2,1,0:T(1,128)S(1)} %get-tuple-element.722), channel_id=1, source_target_pairs={{0,2},{2,4},{4,6},{6,8},{8,10},{10,12},{12,14},{14,16},{16,18},{18... | collective-permute-start | bytes 6152 | tf_op jit(solution)/shard_map/ppermute | solution.py:24
  204.5 6.7 collective-permute-start.15
  257.9 15.9 %collective-permute-start.18 = (f32[2,16,1]{2,1,0:T(8,128)S(1)}, f32[2,16,1]{2,1,0:T(8,128)S(1)}, u32[]{:S(2)}, u32[]{:S(2)}) collective-permute-start(f32[2,16,1]{2,1,0:T(8,128)S(1)} %get-tuple-element.719), channel_id=1, source_target_pairs={{1,0},{3,2},{5,4},{7,6},{9,8},{11,10},{13,12},{15,14},{17,16},{19,... | collective-permute-start | bytes 392 | tf_op jit(solution)/shard_map/ppermute | solution.py:26
  259.2 14.6 %collective-permute-start.16 = (f32[2,1,256]{2,1,0:T(1,128)S(1)}, f32[2,1,256]{2,1,0:T(1,128)S(1)}, u32[]{:S(2)}, u32[]{:S(2)}) collective-permute-start(f32[2,1,256]{2,1,0:T(1,128)S(1)} %get-tuple-element.717), channel_id=1, source_target_pairs={{2,0},{4,2},{6,4},{8,6},{10,8},{12,10},{14,12},{16,14},{18,16},{20... | collective-permute-start | bytes 6152 | tf_op jit(solution)/shard_map/ppermute | solution.py:26
  260.5 13.4 %collective-permute-start.17 = (f32[2,1,256]{2,1,0:T(1,128)S(1)}, f32[2,1,256]{2,1,0:T(1,128)S(1)}, u32[]{:S(2)}, u32[]{:S(2)}) collective-permute-start(f32[2,1,256]{2,1,0:T(1,128)S(1)} %get-tuple-element.718), channel_id=1, source_target_pairs={{0,2},{2,4},{4,6},{6,8},{8,10},{10,12},{12,14},{14,16},{16,18},{18... | collective-permute-start | bytes 6152 | tf_op jit(solution)/shard_map/ppermute | solution.py:24
  267.0 6.8 collective-permute-start.19
  319.7 16.0 %collective-permute-start.22 = (f32[2,16,1]{2,1,0:T(8,128)S(1)}, f32[2,16,1]{2,1,0:T(8,128)S(1)}, u32[]{:S(2)}, u32[]{:S(2)}) collective-permute-start(f32[2,16,1]{2,1,0:T(8,128)S(1)} %get-tuple-element.715), channel_id=1, source_target_pairs={{1,0},{3,2},{5,4},{7,6},{9,8},{11,10},{13,12},{15,14},{17,16},{19,... | collective-permute-start | bytes 392 | tf_op jit(solution)/shard_map/ppermute | solution.py:26
  321.1 14.7 %collective-permute-start.20 = (f32[2,1,256]{2,1,0:T(1,128)S(1)}, f32[2,1,256]{2,1,0:T(1,128)S(1)}, u32[]{:S(2)}, u32[]{:S(2)}) collective-permute-start(f32[2,1,256]{2,1,0:T(1,128)S(1)} %get-tuple-element.713), channel_id=1, source_target_pairs={{2,0},{4,2},{6,4},{8,6},{10,8},{12,10},{14,12},{16,14},{18,16},{20... | collective-permute-start | bytes 6152 | tf_op jit(solution)/shard_map/ppermute | solution.py:26
  322.4 13.4 %collective-permute-start.21 = (f32[2,1,256]{2,1,0:T(1,128)S(1)}, f32[2,1,256]{2,1,0:T(1,128)S(1)}, u32[]{:S(2)}, u32[]{:S(2)}) collective-permute-start(f32[2,1,256]{2,1,0:T(1,128)S(1)} %get-tuple-element.714), channel_id=1, source_target_pairs={{0,2},{2,4},{4,6},{6,8},{8,10},{10,12},{12,14},{14,16},{16,18},{18... | collective-permute-start | bytes 6152 | tf_op jit(solution)/shard_map/ppermute | solution.py:24
  329.1 6.7 collective-permute-start.23
  382.4 15.7 %collective-permute-start.26 = (f32[2,16,1]{2,1,0:T(8,128)S(1)}, f32[2,16,1]{2,1,0:T(8,128)S(1)}, u32[]{:S(2)}, u32[]{:S(2)}) collective-permute-start(f32[2,16,1]{2,1,0:T(8,128)S(1)} %get-tuple-element.711), channel_id=1, source_target_pairs={{1,0},{3,2},{5,4},{7,6},{9,8},{11,10},{13,12},{15,14},{17,16},{19,... | collective-permute-start | bytes 392 | tf_op jit(solution)/shard_map/ppermute | solution.py:26
  383.7 14.4 %collective-permute-start.24 = (f32[2,1,256]{2,1,0:T(1,128)S(1)}, f32[2,1,256]{2,1,0:T(1,128)S(1)}, u32[]{:S(2)}, u32[]{:S(2)}) collective-permute-start(f32[2,1,256]{2,1,0:T(1,128)S(1)} %get-tuple-element.709), channel_id=1, source_target_pairs={{2,0},{4,2},{6,4},{8,6},{10,8},{12,10},{14,12},{16,14},{18,16},{20... | collective-permute-start | bytes 6152 | tf_op jit(solution)/shard_map/ppermute | solution.py:26
  385.0 13.2 %collective-permute-start.25 = (f32[2,1,256]{2,1,0:T(1,128)S(1)}, f32[2,1,256]{2,1,0:T(1,128)S(1)}, u32[]{:S(2)}, u32[]{:S(2)}) collective-permute-start(f32[2,1,256]{2,1,0:T(1,128)S(1)} %get-tuple-element.710), channel_id=1, source_target_pairs={{0,2},{2,4},{4,6},{6,8},{8,10},{10,12},{12,14},{14,16},{16,18},{18... | collective-permute-start | bytes 6152 | tf_op jit(solution)/shard_map/ppermute | solution.py:24
  391.5 6.7 collective-permute-start.27
  444.3 16.0 %collective-permute-start.30 = (f32[2,16,1]{2,1,0:T(8,128)S(1)}, f32[2,16,1]{2,1,0:T(8,128)S(1)}, u32[]{:S(2)}, u32[]{:S(2)}) collective-permute-start(f32[2,16,1]{2,1,0:T(8,128)S(1)} %get-tuple-element.707), channel_id=1, source_target_pairs={{1,0},{3,2},{5,4},{7,6},{9,8},{11,10},{13,12},{15,14},{17,16},{19,... | collective-permute-start | bytes 392 | tf_op jit(solution)/shard_map/ppermute | solution.py:26
  445.6 14.7 %collective-permute-start.28 = (f32[2,1,256]{2,1,0:T(1,128)S(1)}, f32[2,1,256]{2,1,0:T(1,128)S(1)}, u32[]{:S(2)}, u32[]{:S(2)}) collective-permute-start(f32[2,1,256]{2,1,0:T(1,128)S(1)} %get-tuple-element.705), channel_id=1, source_target_pairs={{2,0},{4,2},{6,4},{8,6},{10,8},{12,10},{14,12},{16,14},{18,16},{20... | collective-permute-start | bytes 6152 | tf_op jit(solution)/shard_map/ppermute | solution.py:26
  446.9 13.4 %collective-permute-start.29 = (f32[2,1,256]{2,1,0:T(1,128)S(1)}, f32[2,1,256]{2,1,0:T(1,128)S(1)}, u32[]{:S(2)}, u32[]{:S(2)}) collective-permute-start(f32[2,1,256]{2,1,0:T(1,128)S(1)} %get-tuple-element.706), channel_id=1, source_target_pairs={{0,2},{2,4},{4,6},{6,8},{8,10},{10,12},{12,14},{14,16},{16,18},{18... | collective-permute-start | bytes 6152 | tf_op jit(solution)/shard_map/ppermute | solution.py:24
  453.6 6.7 collective-permute-start.31
  507.4 15.9 %collective-permute-start.34 = (f32[2,16,1]{2,1,0:T(8,128)S(1)}, f32[2,16,1]{2,1,0:T(8,128)S(1)}, u32[]{:S(2)}, u32[]{:S(2)}) collective-permute-start(f32[2,16,1]{2,1,0:T(8,128)S(1)} %get-tuple-element.703), channel_id=1, source_target_pairs={{1,0},{3,2},{5,4},{7,6},{9,8},{11,10},{13,12},{15,14},{17,16},{19,... | collective-permute-start | bytes 392 | tf_op jit(solution)/shard_map/ppermute | solution.py:26
  508.7 14.6 %collective-permute-start.32 = (f32[2,1,256]{2,1,0:T(1,128)S(1)}, f32[2,1,256]{2,1,0:T(1,128)S(1)}, u32[]{:S(2)}, u32[]{:S(2)}) collective-permute-start(f32[2,1,256]{2,1,0:T(1,128)S(1)} %get-tuple-element.701), channel_id=1, source_target_pairs={{2,0},{4,2},{6,4},{8,6},{10,8},{12,10},{14,12},{16,14},{18,16},{20... | collective-permute-start | bytes 6152 | tf_op jit(solution)/shard_map/ppermute | solution.py:26
  510.0 13.3 %collective-permute-start.33 = (f32[2,1,256]{2,1,0:T(1,128)S(1)}, f32[2,1,256]{2,1,0:T(1,128)S(1)}, u32[]{:S(2)}, u32[]{:S(2)}) collective-permute-start(f32[2,1,256]{2,1,0:T(1,128)S(1)} %get-tuple-element.702), channel_id=1, source_target_pairs={{0,2},{2,4},{4,6},{6,8},{8,10},{10,12},{12,14},{14,16},{16,18},{18... | collective-permute-start | bytes 6152 | tf_op jit(solution)/shard_map/ppermute | solution.py:24
  516.6 6.7 collective-permute-start.35
  569.3 15.8 %collective-permute-start.38 = (f32[2,16,1]{2,1,0:T(8,128)S(1)}, f32[2,16,1]{2,1,0:T(8,128)S(1)}, u32[]{:S(2)}, u32[]{:S(2)}) collective-permute-start(f32[2,16,1]{2,1,0:T(8,128)S(1)} %get-tuple-element.699), channel_id=1, source_target_pairs={{1,0},{3,2},{5,4},{7,6},{9,8},{11,10},{13,12},{15,14},{17,16},{19,... | collective-permute-start | bytes 392 | tf_op jit(solution)/shard_map/ppermute | solution.py:26
  570.6 14.5 %collective-permute-start.36 = (f32[2,1,256]{2,1,0:T(1,128)S(1)}, f32[2,1,256]{2,1,0:T(1,128)S(1)}, u32[]{:S(2)}, u32[]{:S(2)}) collective-permute-start(f32[2,1,256]{2,1,0:T(1,128)S(1)} %get-tuple-element.697), channel_id=1, source_target_pairs={{2,0},{4,2},{6,4},{8,6},{10,8},{12,10},{14,12},{16,14},{18,16},{20... | collective-permute-start | bytes 6152 | tf_op jit(solution)/shard_map/ppermute | solution.py:26
  571.9 13.2 %collective-permute-start.37 = (f32[2,1,256]{2,1,0:T(1,128)S(1)}, f32[2,1,256]{2,1,0:T(1,128)S(1)}, u32[]{:S(2)}, u32[]{:S(2)}) collective-permute-start(f32[2,1,256]{2,1,0:T(1,128)S(1)} %get-tuple-element.698), channel_id=1, source_target_pairs={{0,2},{2,4},{4,6},{6,8},{8,10},{10,12},{12,14},{14,16},{16,18},{18... | collective-permute-start | bytes 6152 | tf_op jit(solution)/shard_map/ppermute | solution.py:24
  632.1 15.8 %collective-permute-start.42 = (f32[2,16,1]{2,1,0:T(8,128)S(1)}, f32[2,16,1]{2,1,0:T(8,128)S(1)}, u32[]{:S(2)}, u32[]{:S(2)}) collective-permute-start(f32[2,16,1]{2,1,0:T(8,128)S(1)} %get-tuple-element.695), channel_id=1, source_target_pairs={{1,0},{3,2},{5,4},{7,6},{9,8},{11,10},{13,12},{15,14},{17,16},{19,... | collective-permute-start | bytes 392 | tf_op jit(solution)/shard_map/ppermute | solution.py:26
  633.4 14.5 %collective-permute-start.40 = (f32[2,1,256]{2,1,0:T(1,128)S(1)}, f32[2,1,256]{2,1,0:T(1,128)S(1)}, u32[]{:S(2)}, u32[]{:S(2)}) collective-permute-start(f32[2,1,256]{2,1,0:T(1,128)S(1)} %get-tuple-element.693), channel_id=1, source_target_pairs={{2,0},{4,2},{6,4},{8,6},{10,8},{12,10},{14,12},{16,14},{18,16},{20... | collective-permute-start | bytes 6152 | tf_op jit(solution)/shard_map/ppermute | solution.py:26
  634.7 13.2 %collective-permute-start.41 = (f32[2,1,256]{2,1,0:T(1,128)S(1)}, f32[2,1,256]{2,1,0:T(1,128)S(1)}, u32[]{:S(2)}, u32[]{:S(2)}) collective-permute-start(f32[2,1,256]{2,1,0:T(1,128)S(1)} %get-tuple-element.694), channel_id=1, source_target_pairs={{0,2},{2,4},{4,6},{6,8},{8,10},{10,12},{12,14},{14,16},{16,18},{18... | collective-permute-start | bytes 6152 | tf_op jit(solution)/shard_map/ppermute | solution.py:24
  641.2 6.7 collective-permute-start.43
  694.3 15.9 %collective-permute-start.46 = (f32[2,16,1]{2,1,0:T(8,128)S(1)}, f32[2,16,1]{2,1,0:T(8,128)S(1)}, u32[]{:S(2)}, u32[]{:S(2)}) collective-permute-start(f32[2,16,1]{2,1,0:T(8,128)S(1)} %get-tuple-element.691), channel_id=1, source_target_pairs={{1,0},{3,2},{5,4},{7,6},{9,8},{11,10},{13,12},{15,14},{17,16},{19,... | collective-permute-start | bytes 392 | tf_op jit(solution)/shard_map/ppermute | solution.py:26
  695.6 14.7 %collective-permute-start.44 = (f32[2,1,256]{2,1,0:T(1,128)S(1)}, f32[2,1,256]{2,1,0:T(1,128)S(1)}, u32[]{:S(2)}, u32[]{:S(2)}) collective-permute-start(f32[2,1,256]{2,1,0:T(1,128)S(1)} %get-tuple-element.689), channel_id=1, source_target_pairs={{2,0},{4,2},{6,4},{8,6},{10,8},{12,10},{14,12},{16,14},{18,16},{20... | collective-permute-start | bytes 6152 | tf_op jit(solution)/shard_map/ppermute | solution.py:26
  696.9 13.4 %collective-permute-start.45 = (f32[2,1,256]{2,1,0:T(1,128)S(1)}, f32[2,1,256]{2,1,0:T(1,128)S(1)}, u32[]{:S(2)}, u32[]{:S(2)}) collective-permute-start(f32[2,1,256]{2,1,0:T(1,128)S(1)} %get-tuple-element.690), channel_id=1, source_target_pairs={{0,2},{2,4},{4,6},{6,8},{8,10},{10,12},{12,14},{14,16},{16,18},{18... | collective-permute-start | bytes 6152 | tf_op jit(solution)/shard_map/ppermute | solution.py:24
  703.5 6.7 collective-permute-start.47
  757.1 16.1 %collective-permute-start.50 = (f32[2,16,1]{2,1,0:T(8,128)S(1)}, f32[2,16,1]{2,1,0:T(8,128)S(1)}, u32[]{:S(2)}, u32[]{:S(2)}) collective-permute-start(f32[2,16,1]{2,1,0:T(8,128)S(1)} %get-tuple-element.687), channel_id=1, source_target_pairs={{1,0},{3,2},{5,4},{7,6},{9,8},{11,10},{13,12},{15,14},{17,16},{19,... | collective-permute-start | bytes 392 | tf_op jit(solution)/shard_map/ppermute | solution.py:26
  758.4 14.9 %collective-permute-start.48 = (f32[2,1,256]{2,1,0:T(1,128)S(1)}, f32[2,1,256]{2,1,0:T(1,128)S(1)}, u32[]{:S(2)}, u32[]{:S(2)}) collective-permute-start(f32[2,1,256]{2,1,0:T(1,128)S(1)} %get-tuple-element.685), channel_id=1, source_target_pairs={{2,0},{4,2},{6,4},{8,6},{10,8},{12,10},{14,12},{16,14},{18,16},{20... | collective-permute-start | bytes 6152 | tf_op jit(solution)/shard_map/ppermute | solution.py:26
  759.7 13.6 %collective-permute-start.49 = (f32[2,1,256]{2,1,0:T(1,128)S(1)}, f32[2,1,256]{2,1,0:T(1,128)S(1)}, u32[]{:S(2)}, u32[]{:S(2)}) collective-permute-start(f32[2,1,256]{2,1,0:T(1,128)S(1)} %get-tuple-element.686), channel_id=1, source_target_pairs={{0,2},{2,4},{4,6},{6,8},{8,10},{10,12},{12,14},{14,16},{16,18},{18... | collective-permute-start | bytes 6152 | tf_op jit(solution)/shard_map/ppermute | solution.py:24
  766.2 7.1 collective-permute-start.51
  (17 other events, 55.0 us)
where the time goes:
time: 899 us; the launch traced here: 886 us
  blocking collectives  572 us (64%)
  starting transfers between devices  153 us (17%)
  other arithmetic  52.4 us (6%)
  local copies, waits for them, and re-layouts  48.3 us (5%)
  matrix products  32.9 us (4%)
  between operations  26 us (3%)
    psum x12, blocking collectives, arnoldi(): lax.psum((partial_value, jnp.sum(image * image)), ('sub', 'gx', 'gy'))  499 us
    ppermute x26, starting transfers between devices, padded(): lax.ppermute(tail, axis, [(i, (i + 1) % count) for i in range(ends)])  120 us
    psum x1, blocking collectives, shards(): lax.psum(jnp.sum(forcing * forcing), ('sub', 'gx', 'gy')) + norm_eps  41 us
    another operation x36, other arithmetic  34.7 us
    ppermute x26, starting transfers between devices, padded(): lax.ppermute(head, axis, [((i + 1) % count, i) for i in range(ends)])  33.5 us
    pmax x1, blocking collectives, shards(): column_error = lax.pmax(local_peak, ('sub', 'gx'))  32.4 us
    scatter x23, local copies, waits for them, and re-layouts, arnoldi(): hessenberg.at[:column + 1, column].set(products).at[column + 1, column]  18.1 us
  transfers between devices with their start and end apart: 52, of which 2 were waited for; matrix products, arithmetic and copies ran while one was open for 7% of the time, Pallas kernels for 0%

commit v1 on v0

--- a/solution.py
+++ b/solution.py
@@ -66,7 +66,9 @@
         current = basis[column].reshape(shape)
         image = (dt_total * (wave(current) - stiffness * current)).reshape(-1)
         partial_value = jnp.dot(basis[: column + 1], image, precision=lax.Precision.HIGHEST)
-        products, squared = lax.psum((partial_value, jnp.sum(image * image)), ("sub", "gx", "gy"))
+        products, squared = lax.psum(
+            lax.psum((partial_value, jnp.sum(image * image)), ("gx", "gy")), "sub"
+        )
         image = image - jnp.dot(products, basis[: column + 1], precision=lax.Precision.HIGHEST)
         length = jnp.sqrt(jnp.maximum(squared - jnp.sum(products * products), 0.0) + norm_eps)
         hessenberg = (

time: 899 us -> 713 us (0.79)
  blocking collectives: 572 us -> 388 us
    psum x12 -> x24, blocking collectives: 499 us -> 317 us  [the longest x12 241 us: arnoldi(): lax.psum((partial_value, jnp.sum(image * image)), ('gx', 'gy'))]
  transfers between devices with their start and end apart: 52 -> 52, of which waited for: 2 -> 2; matrix products, arithmetic and copies ran while one was open for 7% -> 8% of each run, Pallas kernels for 0% -> 0%
where the time goes in v1:
time: 713 us; the launch traced here: 702 us
  blocking collectives  388 us (54%)
  starting transfers between devices  153 us (21%)
  other arithmetic  52.4 us (7%)
  local copies, waits for them, and re-layouts  48.3 us (7%)
  matrix products  32.9 us (5%)
  between operations  26 us (4%)
    psum x12, blocking collectives, arnoldi(): lax.psum((partial_value, jnp.sum(image * image)), ('gx', 'gy'))  241 us
    ppermute x26, starting transfers between devices, padded(): lax.ppermute(tail, axis, [(i, (i + 1) % count) for i in range(ends)])  120 us
    psum x12, blocking collectives, arnoldi(): lax.psum(lax.psum((partial_value, jnp.sum(image * image)), ('gx', 'gy')),...  75.8 us
    psum x1, blocking collectives, shards(): lax.psum(jnp.sum(forcing * forcing), ('sub', 'gx', 'gy')) + norm_eps  41 us
    another operation x36, other arithmetic  34.7 us
    ppermute x26, starting transfers between devices, padded(): lax.ppermute(head, axis, [((i + 1) % count, i) for i in range(ends)])  33.5 us
    pmax x1, blocking collectives, shards(): column_error = lax.pmax(local_peak, ('sub', 'gx'))  30.3 us
    scatter x23, local copies, waits for them, and re-layouts, arnoldi(): hessenberg.at[:column + 1, column].set(products).at[column + 1, column]  18.1 us
  transfers between devices with their start and end apart: 52, of which 2 were waited for; matrix products, arithmetic and copies ran while one was open for 8% of the time, Pallas kernels for 0%

profile of v1, /device:TPU:0, one launch (start us, length us, event | category | flops | bytes accessed | tf_op | source)
XLA Modules:
  0.0 701.5 jit_solution(16202814034907362377)
XLA Ops:
  2.7 4.9 collective-permute-start.3
  23.8 5.2 collective-permute-start.1
  33.7 41.0 %psum.343 = f32[]{:T(128)} all-reduce(f32[]{:T(128)} %get-tuple-element.664), channel_id=1, replica_groups=mesh['sub'=4,'gx'=4,'gy'=2] {'sub','gx','gy'}, use_global_device_ids=true, to_apply=%region_1.0 | all-reduce | flops 1 | bytes 8 | tf_op jit(solution)/shard_map/psum | solution.py:84
  77.1 4.7 collective-permute-start.5
  83.1 4.5 collective-permute-start.7
  89.8 22.4 %all-reduce.17 = (f32[]{:T(128)}, f32[1]{0:T(128)}) all-reduce(f32[]{:T(128)} %get-tuple-element.587, f32[1]{0:T(128)} %bitcast.1), channel_id=1, replica_groups=mesh['sub'=4,'gx'=4,'gy'=2] {'gx','gy'}, use_global_device_ids=true, to_apply=%region_5.0 | all-reduce | flops 2 | bytes 16 | tf_op jit(solution)/shard_map/psum | solution.py:70
  112.3 6.4 all-reduce.29
  123.0 4.5 collective-permute-start.9
  128.9 4.5 collective-permute-start.11
  136.9 21.2 %all-reduce.16 = (f32[2]{0:T(128)S(1)}, f32[]{:T(128)}) all-reduce(f32[2]{0:T(128)S(1)} %convolution_bitcast_fusion.10, f32[]{:T(128)} %get-tuple-element.660), channel_id=1, replica_groups=mesh['sub'=4,'gx'=4,'gy'=2] {'gx','gy'}, use_global_device_ids=true, to_apply=%region_8.0 | all-reduce | flops 3 | bytes 24 | tf_op jit(solution)/shard_map/psum | solution.py:70
  158.2 6.3 all-reduce.28
  169.9 4.5 collective-permute-start.13
  176.4 4.5 collective-permute-start.15
  185.2 19.8 %all-reduce.15 = (f32[3]{0:T(128)S(1)}, f32[]{:T(128)}) all-reduce(f32[3]{0:T(128)S(1)} %convolution_bitcast_fusion.9, f32[]{:T(128)} %get-tuple-element.658), channel_id=1, replica_groups=mesh['sub'=4,'gx'=4,'gy'=2] {'gx','gy'}, use_global_device_ids=true, to_apply=%region_15.0 | all-reduce | flops 4 | bytes 32 | tf_op jit(solution)/shard_map/psum | solution.py:70
  205.0 6.3 all-reduce.27
  216.7 4.5 collective-permute-start.17
  223.2 4.5 collective-permute-start.19
  231.9 19.8 %all-reduce.14 = (f32[4]{0:T(128)S(1)}, f32[]{:T(128)}) all-reduce(f32[4]{0:T(128)S(1)} %convolution_bitcast_fusion.8, f32[]{:T(128)} %get-tuple-element.656), channel_id=1, replica_groups=mesh['sub'=4,'gx'=4,'gy'=2] {'gx','gy'}, use_global_device_ids=true, to_apply=%region_22.0 | all-reduce | flops 5 | bytes 40 | tf_op jit(solution)/shard_map/psum | solution.py:70
  251.7 6.7 all-reduce.26
  264.0 4.5 collective-permute-start.21
  270.6 4.5 collective-permute-start.23
  279.3 19.8 %all-reduce.13 = (f32[5]{0:T(128)S(1)}, f32[]{:T(128)}) all-reduce(f32[5]{0:T(128)S(1)} %convolution_bitcast_fusion.7, f32[]{:T(128)} %get-tuple-element.654), channel_id=1, replica_groups=mesh['sub'=4,'gx'=4,'gy'=2] {'gx','gy'}, use_global_device_ids=true, to_apply=%region_29.0 | all-reduce | flops 6 | bytes 48 | tf_op jit(solution)/shard_map/psum | solution.py:70
  299.1 6.3 all-reduce.25
  310.9 4.5 collective-permute-start.25
  317.3 4.5 collective-permute-start.27
  326.0 19.8 %all-reduce.12 = (f32[6]{0:T(128)S(1)}, f32[]{:T(128)}) all-reduce(f32[6]{0:T(128)S(1)} %convolution_bitcast_fusion.6, f32[]{:T(128)} %get-tuple-element.652), channel_id=1, replica_groups=mesh['sub'=4,'gx'=4,'gy'=2] {'gx','gy'}, use_global_device_ids=true, to_apply=%region_36.0 | all-reduce | flops 7 | bytes 56 | tf_op jit(solution)/shard_map/psum | solution.py:70
  345.8 6.3 all-reduce.24
  357.6 4.5 collective-permute-start.29
  364.2 4.5 collective-permute-start.31
  372.9 19.8 %all-reduce.11 = (f32[7]{0:T(128)S(1)}, f32[]{:T(128)}) all-reduce(f32[7]{0:T(128)S(1)} %convolution_bitcast_fusion.5, f32[]{:T(128)} %get-tuple-element.650), channel_id=1, replica_groups=mesh['sub'=4,'gx'=4,'gy'=2] {'gx','gy'}, use_global_device_ids=true, to_apply=%region_43.0 | all-reduce | flops 8 | bytes 64 | tf_op jit(solution)/shard_map/psum | solution.py:70
  392.7 6.3 all-reduce.23
  404.5 4.5 collective-permute-start.33
  411.1 4.5 collective-permute-start.35
  420.0 19.6 %all-reduce.10 = (f32[8]{0:T(128)S(1)}, f32[]{:T(128)}) all-reduce(f32[8]{0:T(128)S(1)} %convolution_bitcast_fusion.4, f32[]{:T(128)} %get-tuple-element.648), channel_id=1, replica_groups=mesh['sub'=4,'gx'=4,'gy'=2] {'gx','gy'}, use_global_device_ids=true, to_apply=%region_50.0 | all-reduce | flops 9 | bytes 72 | tf_op jit(solution)/shard_map/psum | solution.py:70
  439.6 6.3 all-reduce.22
  451.3 4.5 collective-permute-start.37
  466.6 19.8 %all-reduce.9 = (f32[9]{0:T(128)S(1)}, f32[]{:T(128)}) all-reduce(f32[9]{0:T(128)S(1)} %convolution_bitcast_fusion.3, f32[]{:T(128)} %get-tuple-element.646), channel_id=1, replica_groups=mesh['sub'=4,'gx'=4,'gy'=2] {'gx','gy'}, use_global_device_ids=true, to_apply=%region_57.0 | all-reduce | flops 10 | bytes 80 | tf_op jit(solution)/shard_map/psum | solution.py:70
  486.4 6.3 all-reduce.21
  498.3 4.5 collective-permute-start.41
  513.6 19.8 %all-reduce.8 = (f32[10]{0:T(128)S(1)}, f32[]{:T(128)}) all-reduce(f32[10]{0:T(128)S(1)} %convolution_bitcast_fusion.2, f32[]{:T(128)} %get-tuple-element.644), channel_id=1, replica_groups=mesh['sub'=4,'gx'=4,'gy'=2] {'gx','gy'}, use_global_device_ids=true, to_apply=%region_64.0 | all-reduce | flops 11 | bytes 88 | tf_op jit(solution)/shard_map/psum | solution.py:70
  533.4 6.3 all-reduce.20
  545.2 4.5 collective-permute-start.45
  560.6 19.8 %all-reduce.7 = (f32[11]{0:T(128)S(1)}, f32[]{:T(128)}) all-reduce(f32[11]{0:T(128)S(1)} %convolution_bitcast_fusion.1, f32[]{:T(128)} %get-tuple-element.642), channel_id=1, replica_groups=mesh['sub'=4,'gx'=4,'gy'=2] {'gx','gy'}, use_global_device_ids=true, to_apply=%region_71.0 | all-reduce | flops 12 | bytes 96 | tf_op jit(solution)/shard_map/psum | solution.py:70
  580.4 6.3 all-reduce.19
  592.2 4.8 collective-permute-start.49
  608.2 19.4 %all-reduce.6 = (f32[12]{0:T(128)S(1)}, f32[]{:T(128)}) all-reduce(f32[12]{0:T(128)S(1)} %convolution_bitcast_fusion, f32[]{:T(128)} %get-tuple-element.640), channel_id=1, replica_groups=mesh['sub'=4,'gx'=4,'gy'=2] {'gx','gy'}, use_global_device_ids=true, to_apply=%region_78.0 | all-reduce | flops 13 | bytes 104 | tf_op jit(solution)/shard_map/psum | solution.py:70
  627.5 6.3 all-reduce.18
  669.3 30.3 %pmax.7 = f32[4,256]{1,0:T(4,128)} all-reduce(f32[4,256]{1,0:T(4,128)S(1)} %broadcast_multiply_fusion.68), channel_id=1, replica_groups=mesh['sub'=4,'gx'=4,'gy'=2] {'sub','gx'}, use_global_device_ids=true, to_apply=%region_86.0 | all-reduce | flops 1024 | bytes 8192 | tf_op jit(solution)/shard_map/pmax | solution.py:104
  (523 shorter events, 186.0 us)
Async XLA Ops:
  1.4 20.9 %collective-permute-start.2 = (f32[2,16,1]{2,1,0:T(8,128)S(1)}, f32[2,16,1]{2,1,0:T(8,128)S(1)}, u32[]{:S(2)}, u32[]{:S(2)}) collective-permute-start(f32[2,16,1]{2,1,0:T(8,128)S(1)} %get-tuple-element.759), channel_id=1, source_target_pairs={{1,0},{3,2},{5,4},{7,6},{9,8},{11,10},{13,12},{15,14},{17,16},{19,... | collective-permute-start | bytes 392 | tf_op jit(solution)/shard_map/ppermute | solution.py:26
  2.7 19.7 %collective-permute-start.3 = (f32[2,16,1]{2,1,0:T(8,128)S(1)}, f32[2,16,1]{2,1,0:T(8,128)S(1)}, u32[]{:S(2)}, u32[]{:S(2)}) collective-permute-start(f32[2,16,1]{2,1,0:T(8,128)S(1)} %get-tuple-element.760), channel_id=1, source_target_pairs={{0,1},{2,3},{4,5},{6,7},{8,9},{10,11},{12,13},{14,15},{16,17},{18,... | collective-permute-start | bytes 392 | tf_op jit(solution)/shard_map/ppermute | solution.py:24
  22.5 10.5 %collective-permute-start = (f32[2,1,256]{2,1,0:T(1,128)S(1)}, f32[2,1,256]{2,1,0:T(1,128)S(1)}, u32[]{:S(2)}, u32[]{:S(2)}) collective-permute-start(f32[2,1,256]{2,1,0:T(1,128)S(1)} %get-tuple-element.757), channel_id=1, source_target_pairs={{2,0},{4,2},{6,4},{8,6},{10,8},{12,10},{14,12},{16,14},{18,16},{20... | collective-permute-start | bytes 6152 | tf_op jit(solution)/shard_map/ppermute | solution.py:26
  23.8 9.2 %collective-permute-start.1 = (f32[2,1,256]{2,1,0:T(1,128)S(1)}, f32[2,1,256]{2,1,0:T(1,128)S(1)}, u32[]{:S(2)}, u32[]{:S(2)}) collective-permute-start(f32[2,1,256]{2,1,0:T(1,128)S(1)} %get-tuple-element.758), channel_id=1, source_target_pairs={{0,2},{2,4},{4,6},{6,8},{8,10},{10,12},{12,14},{14,16},{16,18},{18... | collective-permute-start | bytes 6152 | tf_op jit(solution)/shard_map/ppermute | solution.py:24
  75.8 13.3 %collective-permute-start.4 = (f32[2,1,256]{2,1,0:T(1,128)S(1)}, f32[2,1,256]{2,1,0:T(1,128)S(1)}, u32[]{:S(2)}, u32[]{:S(2)}) collective-permute-start(f32[2,1,256]{2,1,0:T(1,128)S(1)} %get-tuple-element.753), channel_id=1, source_target_pairs={{2,0},{4,2},{6,4},{8,6},{10,8},{12,10},{14,12},{16,14},{18,16},{20... | collective-permute-start | bytes 6152 | tf_op jit(solution)/shard_map/ppermute | solution.py:26
  77.1 12.0 %collective-permute-start.5 = (f32[2,1,256]{2,1,0:T(1,128)S(1)}, f32[2,1,256]{2,1,0:T(1,128)S(1)}, u32[]{:S(2)}, u32[]{:S(2)}) collective-permute-start(f32[2,1,256]{2,1,0:T(1,128)S(1)} %get-tuple-element.754), channel_id=1, source_target_pairs={{0,2},{2,4},{4,6},{6,8},{8,10},{10,12},{12,14},{14,16},{16,18},{18... | collective-permute-start | bytes 6152 | tf_op jit(solution)/shard_map/ppermute | solution.py:24
  121.7 13.2 %collective-permute-start.8 = (f32[2,1,256]{2,1,0:T(1,128)S(1)}, f32[2,1,256]{2,1,0:T(1,128)S(1)}, u32[]{:S(2)}, u32[]{:S(2)}) collective-permute-start(f32[2,1,256]{2,1,0:T(1,128)S(1)} %get-tuple-element.749), channel_id=1, source_target_pairs={{2,0},{4,2},{6,4},{8,6},{10,8},{12,10},{14,12},{16,14},{18,16},{20... | collective-permute-start | bytes 6152 | tf_op jit(solution)/shard_map/ppermute | solution.py:26
  123.0 11.9 %collective-permute-start.9 = (f32[2,1,256]{2,1,0:T(1,128)S(1)}, f32[2,1,256]{2,1,0:T(1,128)S(1)}, u32[]{:S(2)}, u32[]{:S(2)}) collective-permute-start(f32[2,1,256]{2,1,0:T(1,128)S(1)} %get-tuple-element.750), channel_id=1, source_target_pairs={{0,2},{2,4},{4,6},{6,8},{8,10},{10,12},{12,14},{14,16},{16,18},{18... | collective-permute-start | bytes 6152 | tf_op jit(solution)/shard_map/ppermute | solution.py:24
  127.6 7.2 %collective-permute-start.10 = (f32[2,16,1]{2,1,0:T(8,128)S(1)}, f32[2,16,1]{2,1,0:T(8,128)S(1)}, u32[]{:S(2)}, u32[]{:S(2)}) collective-permute-start(f32[2,16,1]{2,1,0:T(8,128)S(1)} %get-tuple-element.751), channel_id=1, source_target_pairs={{1,0},{3,2},{5,4},{7,6},{9,8},{11,10},{13,12},{15,14},{17,16},{19,... | collective-permute-start | bytes 392 | tf_op jit(solution)/shard_map/ppermute | solution.py:26
  167.3 15.8 %collective-permute-start.14 = (f32[2,16,1]{2,1,0:T(8,128)S(1)}, f32[2,16,1]{2,1,0:T(8,128)S(1)}, u32[]{:S(2)}, u32[]{:S(2)}) collective-permute-start(f32[2,16,1]{2,1,0:T(8,128)S(1)} %get-tuple-element.747), channel_id=1, source_target_pairs={{1,0},{3,2},{5,4},{7,6},{9,8},{11,10},{13,12},{15,14},{17,16},{19,... | collective-permute-start | bytes 392 | tf_op jit(solution)/shard_map/ppermute | solution.py:26
  168.6 14.5 %collective-permute-start.12 = (f32[2,1,256]{2,1,0:T(1,128)S(1)}, f32[2,1,256]{2,1,0:T(1,128)S(1)}, u32[]{:S(2)}, u32[]{:S(2)}) collective-permute-start(f32[2,1,256]{2,1,0:T(1,128)S(1)} %get-tuple-element.745), channel_id=1, source_target_pairs={{2,0},{4,2},{6,4},{8,6},{10,8},{12,10},{14,12},{16,14},{18,16},{20... | collective-permute-start | bytes 6152 | tf_op jit(solution)/shard_map/ppermute | solution.py:26
  169.9 13.2 %collective-permute-start.13 = (f32[2,1,256]{2,1,0:T(1,128)S(1)}, f32[2,1,256]{2,1,0:T(1,128)S(1)}, u32[]{:S(2)}, u32[]{:S(2)}) collective-permute-start(f32[2,1,256]{2,1,0:T(1,128)S(1)} %get-tuple-element.746), channel_id=1, source_target_pairs={{0,2},{2,4},{4,6},{6,8},{8,10},{10,12},{12,14},{14,16},{16,18},{18... | collective-permute-start | bytes 6152 | tf_op jit(solution)/shard_map/ppermute | solution.py:24
  176.4 6.7 collective-permute-start.15
  214.1 15.7 %collective-permute-start.18 = (f32[2,16,1]{2,1,0:T(8,128)S(1)}, f32[2,16,1]{2,1,0:T(8,128)S(1)}, u32[]{:S(2)}, u32[]{:S(2)}) collective-permute-start(f32[2,16,1]{2,1,0:T(8,128)S(1)} %get-tuple-element.743), channel_id=1, source_target_pairs={{1,0},{3,2},{5,4},{7,6},{9,8},{11,10},{13,12},{15,14},{17,16},{19,... | collective-permute-start | bytes 392 | tf_op jit(solution)/shard_map/ppermute | solution.py:26
  215.4 14.5 %collective-permute-start.16 = (f32[2,1,256]{2,1,0:T(1,128)S(1)}, f32[2,1,256]{2,1,0:T(1,128)S(1)}, u32[]{:S(2)}, u32[]{:S(2)}) collective-permute-start(f32[2,1,256]{2,1,0:T(1,128)S(1)} %get-tuple-element.741), channel_id=1, source_target_pairs={{2,0},{4,2},{6,4},{8,6},{10,8},{12,10},{14,12},{16,14},{18,16},{20... | collective-permute-start | bytes 6152 | tf_op jit(solution)/shard_map/ppermute | solution.py:26
  216.7 13.2 %collective-permute-start.17 = (f32[2,1,256]{2,1,0:T(1,128)S(1)}, f32[2,1,256]{2,1,0:T(1,128)S(1)}, u32[]{:S(2)}, u32[]{:S(2)}) collective-permute-start(f32[2,1,256]{2,1,0:T(1,128)S(1)} %get-tuple-element.742), channel_id=1, source_target_pairs={{0,2},{2,4},{4,6},{6,8},{8,10},{10,12},{12,14},{14,16},{16,18},{18... | collective-permute-start | bytes 6152 | tf_op jit(solution)/shard_map/ppermute | solution.py:24
  223.2 6.7 collective-permute-start.19
  261.4 15.9 %collective-permute-start.22 = (f32[2,16,1]{2,1,0:T(8,128)S(1)}, f32[2,16,1]{2,1,0:T(8,128)S(1)}, u32[]{:S(2)}, u32[]{:S(2)}) collective-permute-start(f32[2,16,1]{2,1,0:T(8,128)S(1)} %get-tuple-element.739), channel_id=1, source_target_pairs={{1,0},{3,2},{5,4},{7,6},{9,8},{11,10},{13,12},{15,14},{17,16},{19,... | collective-permute-start | bytes 392 | tf_op jit(solution)/shard_map/ppermute | solution.py:26
  262.7 14.6 %collective-permute-start.20 = (f32[2,1,256]{2,1,0:T(1,128)S(1)}, f32[2,1,256]{2,1,0:T(1,128)S(1)}, u32[]{:S(2)}, u32[]{:S(2)}) collective-permute-start(f32[2,1,256]{2,1,0:T(1,128)S(1)} %get-tuple-element.737), channel_id=1, source_target_pairs={{2,0},{4,2},{6,4},{8,6},{10,8},{12,10},{14,12},{16,14},{18,16},{20... | collective-permute-start | bytes 6152 | tf_op jit(solution)/shard_map/ppermute | solution.py:26
  264.0 13.3 %collective-permute-start.21 = (f32[2,1,256]{2,1,0:T(1,128)S(1)}, f32[2,1,256]{2,1,0:T(1,128)S(1)}, u32[]{:S(2)}, u32[]{:S(2)}) collective-permute-start(f32[2,1,256]{2,1,0:T(1,128)S(1)} %get-tuple-element.738), channel_id=1, source_target_pairs={{0,2},{2,4},{4,6},{6,8},{8,10},{10,12},{12,14},{14,16},{16,18},{18... | collective-permute-start | bytes 6152 | tf_op jit(solution)/shard_map/ppermute | solution.py:24
  270.6 6.7 collective-permute-start.23
  308.2 15.7 %collective-permute-start.26 = (f32[2,16,1]{2,1,0:T(8,128)S(1)}, f32[2,16,1]{2,1,0:T(8,128)S(1)}, u32[]{:S(2)}, u32[]{:S(2)}) collective-permute-start(f32[2,16,1]{2,1,0:T(8,128)S(1)} %get-tuple-element.735), channel_id=1, source_target_pairs={{1,0},{3,2},{5,4},{7,6},{9,8},{11,10},{13,12},{15,14},{17,16},{19,... | collective-permute-start | bytes 392 | tf_op jit(solution)/shard_map/ppermute | solution.py:26
  309.6 14.4 %collective-permute-start.24 = (f32[2,1,256]{2,1,0:T(1,128)S(1)}, f32[2,1,256]{2,1,0:T(1,128)S(1)}, u32[]{:S(2)}, u32[]{:S(2)}) collective-permute-start(f32[2,1,256]{2,1,0:T(1,128)S(1)} %get-tuple-element.733), channel_id=1, source_target_pairs={{2,0},{4,2},{6,4},{8,6},{10,8},{12,10},{14,12},{16,14},{18,16},{20... | collective-permute-start | bytes 6152 | tf_op jit(solution)/shard_map/ppermute | solution.py:26
  310.9 13.2 %collective-permute-start.25 = (f32[2,1,256]{2,1,0:T(1,128)S(1)}, f32[2,1,256]{2,1,0:T(1,128)S(1)}, u32[]{:S(2)}, u32[]{:S(2)}) collective-permute-start(f32[2,1,256]{2,1,0:T(1,128)S(1)} %get-tuple-element.734), channel_id=1, source_target_pairs={{0,2},{2,4},{4,6},{6,8},{8,10},{10,12},{12,14},{14,16},{16,18},{18... | collective-permute-start | bytes 6152 | tf_op jit(solution)/shard_map/ppermute | solution.py:24
  317.3 6.7 collective-permute-start.27
  355.0 15.9 %collective-permute-start.30 = (f32[2,16,1]{2,1,0:T(8,128)S(1)}, f32[2,16,1]{2,1,0:T(8,128)S(1)}, u32[]{:S(2)}, u32[]{:S(2)}) collective-permute-start(f32[2,16,1]{2,1,0:T(8,128)S(1)} %get-tuple-element.731), channel_id=1, source_target_pairs={{1,0},{3,2},{5,4},{7,6},{9,8},{11,10},{13,12},{15,14},{17,16},{19,... | collective-permute-start | bytes 392 | tf_op jit(solution)/shard_map/ppermute | solution.py:26
  356.3 14.6 %collective-permute-start.28 = (f32[2,1,256]{2,1,0:T(1,128)S(1)}, f32[2,1,256]{2,1,0:T(1,128)S(1)}, u32[]{:S(2)}, u32[]{:S(2)}) collective-permute-start(f32[2,1,256]{2,1,0:T(1,128)S(1)} %get-tuple-element.729), channel_id=1, source_target_pairs={{2,0},{4,2},{6,4},{8,6},{10,8},{12,10},{14,12},{16,14},{18,16},{20... | collective-permute-start | bytes 6152 | tf_op jit(solution)/shard_map/ppermute | solution.py:26
  357.6 13.3 %collective-permute-start.29 = (f32[2,1,256]{2,1,0:T(1,128)S(1)}, f32[2,1,256]{2,1,0:T(1,128)S(1)}, u32[]{:S(2)}, u32[]{:S(2)}) collective-permute-start(f32[2,1,256]{2,1,0:T(1,128)S(1)} %get-tuple-element.730), channel_id=1, source_target_pairs={{0,2},{2,4},{4,6},{6,8},{8,10},{10,12},{12,14},{14,16},{16,18},{18... | collective-permute-start | bytes 6152 | tf_op jit(solution)/shard_map/ppermute | solution.py:24
  364.2 6.7 collective-permute-start.31
  401.9 16.0 %collective-permute-start.34 = (f32[2,16,1]{2,1,0:T(8,128)S(1)}, f32[2,16,1]{2,1,0:T(8,128)S(1)}, u32[]{:S(2)}, u32[]{:S(2)}) collective-permute-start(f32[2,16,1]{2,1,0:T(8,128)S(1)} %get-tuple-element.727), channel_id=1, source_target_pairs={{1,0},{3,2},{5,4},{7,6},{9,8},{11,10},{13,12},{15,14},{17,16},{19,... | collective-permute-start | bytes 392 | tf_op jit(solution)/shard_map/ppermute | solution.py:26
  403.2 14.8 %collective-permute-start.32 = (f32[2,1,256]{2,1,0:T(1,128)S(1)}, f32[2,1,256]{2,1,0:T(1,128)S(1)}, u32[]{:S(2)}, u32[]{:S(2)}) collective-permute-start(f32[2,1,256]{2,1,0:T(1,128)S(1)} %get-tuple-element.725), channel_id=1, source_target_pairs={{2,0},{4,2},{6,4},{8,6},{10,8},{12,10},{14,12},{16,14},{18,16},{20... | collective-permute-start | bytes 6152 | tf_op jit(solution)/shard_map/ppermute | solution.py:26
  404.5 13.5 %collective-permute-start.33 = (f32[2,1,256]{2,1,0:T(1,128)S(1)}, f32[2,1,256]{2,1,0:T(1,128)S(1)}, u32[]{:S(2)}, u32[]{:S(2)}) collective-permute-start(f32[2,1,256]{2,1,0:T(1,128)S(1)} %get-tuple-element.726), channel_id=1, source_target_pairs={{0,2},{2,4},{4,6},{6,8},{8,10},{10,12},{12,14},{14,16},{16,18},{18... | collective-permute-start | bytes 6152 | tf_op jit(solution)/shard_map/ppermute | solution.py:24
  411.1 6.9 collective-permute-start.35
  448.7 15.7 %collective-permute-start.38 = (f32[2,16,1]{2,1,0:T(8,128)S(1)}, f32[2,16,1]{2,1,0:T(8,128)S(1)}, u32[]{:S(2)}, u32[]{:S(2)}) collective-permute-start(f32[2,16,1]{2,1,0:T(8,128)S(1)} %get-tuple-element.723), channel_id=1, source_target_pairs={{1,0},{3,2},{5,4},{7,6},{9,8},{11,10},{13,12},{15,14},{17,16},{19,... | collective-permute-start | bytes 392 | tf_op jit(solution)/shard_map/ppermute | solution.py:26
  450.0 14.4 %collective-permute-start.36 = (f32[2,1,256]{2,1,0:T(1,128)S(1)}, f32[2,1,256]{2,1,0:T(1,128)S(1)}, u32[]{:S(2)}, u32[]{:S(2)}) collective-permute-start(f32[2,1,256]{2,1,0:T(1,128)S(1)} %get-tuple-element.721), channel_id=1, source_target_pairs={{2,0},{4,2},{6,4},{8,6},{10,8},{12,10},{14,12},{16,14},{18,16},{20... | collective-permute-start | bytes 6152 | tf_op jit(solution)/shard_map/ppermute | solution.py:26
  451.3 13.1 %collective-permute-start.37 = (f32[2,1,256]{2,1,0:T(1,128)S(1)}, f32[2,1,256]{2,1,0:T(1,128)S(1)}, u32[]{:S(2)}, u32[]{:S(2)}) collective-permute-start(f32[2,1,256]{2,1,0:T(1,128)S(1)} %get-tuple-element.722), channel_id=1, source_target_pairs={{0,2},{2,4},{4,6},{6,8},{8,10},{10,12},{12,14},{14,16},{16,18},{18... | collective-permute-start | bytes 6152 | tf_op jit(solution)/shard_map/ppermute | solution.py:24
  495.6 15.8 %collective-permute-start.42 = (f32[2,16,1]{2,1,0:T(8,128)S(1)}, f32[2,16,1]{2,1,0:T(8,128)S(1)}, u32[]{:S(2)}, u32[]{:S(2)}) collective-permute-start(f32[2,16,1]{2,1,0:T(8,128)S(1)} %get-tuple-element.719), channel_id=1, source_target_pairs={{1,0},{3,2},{5,4},{7,6},{9,8},{11,10},{13,12},{15,14},{17,16},{19,... | collective-permute-start | bytes 392 | tf_op jit(solution)/shard_map/ppermute | solution.py:26
  497.0 14.5 %collective-permute-start.40 = (f32[2,1,256]{2,1,0:T(1,128)S(1)}, f32[2,1,256]{2,1,0:T(1,128)S(1)}, u32[]{:S(2)}, u32[]{:S(2)}) collective-permute-start(f32[2,1,256]{2,1,0:T(1,128)S(1)} %get-tuple-element.717), channel_id=1, source_target_pairs={{2,0},{4,2},{6,4},{8,6},{10,8},{12,10},{14,12},{16,14},{18,16},{20... | collective-permute-start | bytes 6152 | tf_op jit(solution)/shard_map/ppermute | solution.py:26
  498.3 13.2 %collective-permute-start.41 = (f32[2,1,256]{2,1,0:T(1,128)S(1)}, f32[2,1,256]{2,1,0:T(1,128)S(1)}, u32[]{:S(2)}, u32[]{:S(2)}) collective-permute-start(f32[2,1,256]{2,1,0:T(1,128)S(1)} %get-tuple-element.718), channel_id=1, source_target_pairs={{0,2},{2,4},{4,6},{6,8},{8,10},{10,12},{12,14},{14,16},{16,18},{18... | collective-permute-start | bytes 6152 | tf_op jit(solution)/shard_map/ppermute | solution.py:24
  504.8 6.7 collective-permute-start.43
  542.6 15.8 %collective-permute-start.46 = (f32[2,16,1]{2,1,0:T(8,128)S(1)}, f32[2,16,1]{2,1,0:T(8,128)S(1)}, u32[]{:S(2)}, u32[]{:S(2)}) collective-permute-start(f32[2,16,1]{2,1,0:T(8,128)S(1)} %get-tuple-element.715), channel_id=1, source_target_pairs={{1,0},{3,2},{5,4},{7,6},{9,8},{11,10},{13,12},{15,14},{17,16},{19,... | collective-permute-start | bytes 392 | tf_op jit(solution)/shard_map/ppermute | solution.py:26
  543.9 14.5 %collective-permute-start.44 = (f32[2,1,256]{2,1,0:T(1,128)S(1)}, f32[2,1,256]{2,1,0:T(1,128)S(1)}, u32[]{:S(2)}, u32[]{:S(2)}) collective-permute-start(f32[2,1,256]{2,1,0:T(1,128)S(1)} %get-tuple-element.713), channel_id=1, source_target_pairs={{2,0},{4,2},{6,4},{8,6},{10,8},{12,10},{14,12},{16,14},{18,16},{20... | collective-permute-start | bytes 6152 | tf_op jit(solution)/shard_map/ppermute | solution.py:26
  545.2 13.3 %collective-permute-start.45 = (f32[2,1,256]{2,1,0:T(1,128)S(1)}, f32[2,1,256]{2,1,0:T(1,128)S(1)}, u32[]{:S(2)}, u32[]{:S(2)}) collective-permute-start(f32[2,1,256]{2,1,0:T(1,128)S(1)} %get-tuple-element.714), channel_id=1, source_target_pairs={{0,2},{2,4},{4,6},{6,8},{8,10},{10,12},{12,14},{14,16},{16,18},{18... | collective-permute-start | bytes 6152 | tf_op jit(solution)/shard_map/ppermute | solution.py:24
  551.8 6.7 collective-permute-start.47
  589.6 16.4 %collective-permute-start.50 = (f32[2,16,1]{2,1,0:T(8,128)S(1)}, f32[2,16,1]{2,1,0:T(8,128)S(1)}, u32[]{:S(2)}, u32[]{:S(2)}) collective-permute-start(f32[2,16,1]{2,1,0:T(8,128)S(1)} %get-tuple-element.711), channel_id=1, source_target_pairs={{1,0},{3,2},{5,4},{7,6},{9,8},{11,10},{13,12},{15,14},{17,16},{19,... | collective-permute-start | bytes 392 | tf_op jit(solution)/shard_map/ppermute | solution.py:26
  590.9 15.1 %collective-permute-start.48 = (f32[2,1,256]{2,1,0:T(1,128)S(1)}, f32[2,1,256]{2,1,0:T(1,128)S(1)}, u32[]{:S(2)}, u32[]{:S(2)}) collective-permute-start(f32[2,1,256]{2,1,0:T(1,128)S(1)} %get-tuple-element.709), channel_id=1, source_target_pairs={{2,0},{4,2},{6,4},{8,6},{10,8},{12,10},{14,12},{16,14},{18,16},{20... | collective-permute-start | bytes 6152 | tf_op jit(solution)/shard_map/ppermute | solution.py:26
  592.2 13.8 %collective-permute-start.49 = (f32[2,1,256]{2,1,0:T(1,128)S(1)}, f32[2,1,256]{2,1,0:T(1,128)S(1)}, u32[]{:S(2)}, u32[]{:S(2)}) collective-permute-start(f32[2,1,256]{2,1,0:T(1,128)S(1)} %get-tuple-element.710), channel_id=1, source_target_pairs={{0,2},{2,4},{4,6},{6,8},{8,10},{10,12},{12,14},{14,16},{16,18},{18... | collective-permute-start | bytes 6152 | tf_op jit(solution)/shard_map/ppermute | solution.py:24
  598.9 7.1 %collective-permute-start.51 = (f32[2,16,1]{2,1,0:T(8,128)S(1)}, f32[2,16,1]{2,1,0:T(8,128)S(1)}, u32[]{:S(2)}, u32[]{:S(2)}) collective-permute-start(f32[2,16,1]{2,1,0:T(8,128)S(1)} %get-tuple-element.712), channel_id=1, source_target_pairs={{0,1},{2,3},{4,5},{6,7},{8,9},{10,11},{12,13},{14,15},{16,17},{18,... | collective-permute-start | bytes 392 | tf_op jit(solution)/shard_map/ppermute | solution.py:24
  (17 other events, 55.0 us)
